TPU v7x, 32 devices: a whole 2x2x4 slice. The times are simulated.
32 devices in a mesh: section: 4 (over y, x), chan: 8 (over z, core).
Axes of the slice: x: 2, y: 2, z: 4, core: 2. Of those that a mesh axis runs over, the one named last changes fastest.
Arguments:
- voltages: bfloat16 [2, 512, 524288], P(None, 'chan', 'section'), may hold values from -6 to 6
- usable: int32 [4096, 512], P(('section', 'chan')), may hold values 0 or 1
- auto_power: float32 [4096, 512], P(('section', 'chan')), may hold values from 0.5 to 4
Outputs:
- gains: float32 [2, 4096, 512], P(None, ('section', 'chan'))
Inputs may be any that keep to these rules, and one draw needn't show every extreme that they name: 1 marks a feed as usable in that channel, 0 as flagged.
All inputs are finite; a program needn't handle non-finite values. No bound on the sum of `usable` on one device may be relied on, other than what follows from the above.
Results may differ from a plain program's by a relative error of at most 0.0046.
Values may be sent and summed in bfloat16 or wider, within the bound.
A program may use at most 576 MiB of HBM per device.

v0:
```python
import math
import jax
import jax.numpy as jnp
from jax import lax
from jax.sharding import PartitionSpec as P

CHANNELS = 4096
TAPS = 4
ITERS = 5
LANES = 128
epsilon = 1e-06


def shifted_2(block, axis, distance):
    devices = range(lax.axis_size(axis))
    route = [(i - distance, i) for i in devices if i - distance in devices]
    return lax.ppermute(block, axis, route)


def prototype(tap_count, channels):
    position = lax.iota(jnp.float32, tap_count * channels)
    offset = (position - 0.5 * tap_count * channels + 0.5) / channels
    window = 0.5 - 0.5 * jnp.cos(2.0 * jnp.pi * (position + 0.5) / (tap_count * channels))
    return (jnp.sin(jnp.pi * offset) / (jnp.pi * offset) * window).reshape(tap_count, channels)


def first_table(outer):
    index = lax.iota(jnp.int32, outer)
    angles = (index[:, None] * index[None, :] % outer).astype(jnp.float32) * (2.0 * math.pi / outer)
    cosine, sine = (jnp.cos(angles), jnp.sin(angles))
    return jnp.stack(
        [jnp.stack([cosine, -sine], axis=1), jnp.stack([sine, cosine], axis=1)], axis=0
    )


def second_table(outer, inner, factor):
    k = lax.iota(jnp.int32, outer)[:, None, None]
    n = lax.iota(jnp.int32, inner)[None, :, None]
    j = lax.iota(jnp.int32, inner)[None, None, :]
    length = outer * inner
    angles = (n * (j * outer + k) % length).astype(jnp.float32) * (2.0 * math.pi / length)
    cosine, sine = (jnp.cos(angles) * factor, jnp.sin(angles) * factor)
    return jnp.stack(
        [jnp.stack([cosine, -sine], axis=2), jnp.stack([sine, cosine], axis=2)], axis=1
    )


def channelize(voltages, history):
    feeds_here = voltages.shape[1]
    blocks = voltages.shape[2] // CHANNELS
    outer = CHANNELS // LANES
    extended = jnp.concatenate([history, voltages], axis=2)
    extended = extended.reshape(2, feeds_here, blocks + TAPS - 1, outer, LANES)
    extended = extended.transpose(0, 3, 2, 1, 4).astype(jnp.float32)
    coeffs = prototype(TAPS, CHANNELS).reshape(TAPS, 1, outer, 1, 1, LANES)
    filtered = coeffs[0] * extended[:, :, 0:blocks]
    for tap_index in range(1, TAPS):
        filtered = filtered + coeffs[tap_index] * extended[:, :, tap_index : tap_index + blocks]
    halfway = jnp.einsum(
        "pmbfn,pmqk->kqbfn", filtered, first_table(outer), precision=lax.Precision.HIGH
    )
    table = second_table(outer, LANES, 1.0 / math.sqrt(CHANNELS))
    spectra = jnp.einsum("kqbfn,kqnrj->krbfj", halfway, table, precision=lax.Precision.HIGH)
    return spectra.astype(jnp.bfloat16)


def local(voltages, usable, auto_power):
    outer = CHANNELS // LANES
    margin = (TAPS - 1) * CHANNELS
    tail_samples = voltages[:, :, voltages.shape[2] - margin :]
    history = shifted_2(tail_samples, "section", 1)
    small = jnp.stack([usable.astype(jnp.float32), auto_power], axis=0)
    small = lax.all_to_all(small, "chan", split_axis=2, concat_axis=1, tiled=True)
    small = lax.all_gather(small, "section", axis=1, tiled=True)
    feeds_here = small.shape[2]
    small = small.reshape(2, LANES, outer, feeds_here).transpose(0, 2, 3, 1)
    weight, power = (small[0], small[1])
    spectra = channelize(voltages, history)
    blocks = spectra.shape[2]
    real = spectra[:, 0].astype(jnp.float32)
    imag = spectra[:, 1].astype(jnp.float32)
    shifted = blocks * power - jnp.sum(real * real + imag * imag, axis=1)
    now_r, now_i = (weight, jnp.zeros_like(weight))
    for iteration in range(ITERS):
        ur, ui = (now_r[:, None], now_i[:, None])
        proj_r = jnp.sum(real * ur + imag * ui, axis=2)
        proj_i = jnp.sum(real * ui - imag * ur, axis=2)
        rows = [proj_r, proj_i]
        if iteration > 0:
            rows.append(jnp.sum(now_r * now_r + now_i * now_i, axis=1)[:, None])
        rows = lax.psum(jnp.concatenate(rows, axis=1), "chan")
        if iteration > 0:
            inverse = 1.0 / jnp.sqrt(rows[:, 2 * blocks :] + epsilon)
            rows = rows[:, : 2 * blocks] * inverse
            now_r, now_i = (now_r * inverse, now_i * inverse)
        pr, pi = (rows[:, :blocks, None], rows[:, blocks:, None])
        back_r = jnp.sum(real * pr - imag * pi, axis=1)
        back_i = jnp.sum(real * pi + imag * pr, axis=1)
        back_r = weight * (back_r + shifted * (weight * now_r))
        back_i = weight * (back_i + shifted * (weight * now_i))
        result = jnp.stack([back_r, back_i], axis=0)
        if iteration < ITERS - 1:
            now_r, now_i = lax.psum(result, "section")
    result = result.transpose(0, 3, 1, 2).reshape(2, CHANNELS, feeds_here)
    result = lax.psum_scatter(result, "section", scatter_dimension=1, tiled=True)
    result = lax.all_to_all(result, "chan", split_axis=1, concat_axis=2, tiled=True)
    length = jnp.sqrt(jnp.sum(result * result, axis=(0, 2)) + epsilon)
    return result / jnp.sqrt(length)[None, :, None]


def solution(mesh):
    in_specs = (
        P(None, "chan", "section"),
        P(("section", "chan"), None),
        P(("section", "chan"), None),
    )
    out_specs = P(None, ("section", "chan"), None)
    return jax.shard_map(local, mesh=mesh, in_specs=in_specs, out_specs=out_specs, check_vma=False)
```

profile of v0, /device:TPU:0, one launch (start us, length us, event | category | flops | bytes accessed | tf_op | source)
XLA Modules:
  0.0 1319.0 jit_solution(3367526858844399999)
XLA Ops:
  10.3 6.6 collective-permute-start
  20.4 4.9 all-to-all-start
  26.0 8.4 fusion.81
  34.4 4.4 maximum_bitcast_fusion.2
  41.7 58.0 %collective-permute-done = bf16[2,64,12288]{2,1,0:T(8,128)(2,1)} collective-permute-done((bf16[2,64,12288]{2,1,0:T(8,128)(2,1)}, bf16[2,64,12288]{2,1,0:T(8,128)(2,1)}, u32[]{:S(2)}, u32[]{:S(2)}) %collective-permute-start) | collective-permute-done | bytes 3145760 | tf_op jit(solution)/shard_map/ppermute | solution.py:17
  99.7 35.9 %maximum_convert_fusion = f32[2,64,143360]{2,1,0:T(8,128)} fusion(bf16[2,64,131072]{2,1,0:T(8,128)(2,1)} %param.3, bf16[2,64,12288]{2,1,0:T(8,128)(2,1)} %collective-permute-done), kind=kLoop, calls=%fused_computation.55 | loop fusion | flops 73400320 | bytes 110100480 | tf_op jit(solution)/shard_map/convert_element_type | solution.py:54
  135.7 48.6 %copy.67 = f32[16,8,1120,128]{3,2,1,0:T(8,128)} copy(f32[16,8,1120,128]{3,1,2,0:T(8,128)} %bitcast.80) | data formatting | bytes 146800640
  184.3 47.7 %copy.76 = f32[2,64,35,32,128]{4,3,0,1,2:T(8,128)} copy(f32[2,64,35,32,128]{4,3,2,1,0:T(8,128)} %bitcast.82) | data formatting | bytes 146800640 | tf_op jit(solution)/shard_map/convert_element_type | solution.py:54
  232.0 112.2 %fusion.57 = f32[32,2,32,64,128,1]{4,0,3,2,1,5:T(8,128)} fusion(f32[2,32,35,64,128]{4,1,0,3,2:T(8,128)} %bitcast.269, f32[32,128]{1,0:T(8,128)S(1)} %get-tuple-element.57, f32[32,128]{1,0:T(8,128)S(1)} %get-tuple-element.58, f32[32,128]{1,0:T(8,128)S(1)} %get-tuple-element.59, f32[32,128]{1,0:T(8,128)S(1)} %get-tuple-element.56, ...), kind=kOutput, calls=%fused_computation.103 | convolution fusion | flops 6559895552 | bytes 335626240 | tf_op jit(solution)/shard_map/pmbfn,pmqk->kqbfn/dot_general | solution.py:59
  344.3 65.4 %fusion.10 = bf16[32,2,32,64,128]{4,3,2,1,0:T(8,128)(2,1)} fusion(f32[32,2,32,64,128,1]{4,0,3,2,1,5:T(8,128)} %fusion.57, f32[32,1,128,2,128]{4,2,1,3,0:T(8,128)} %get-tuple-element.45, f32[32,1,128,2,128]{4,2,1,3,0:T(8,128)} %get-tuple-element.44), kind=kOutput, calls=%fused_computation.56 | convolution fusion | flops 25788678144 | bytes 109051904 | tf_op jit(solution)/shard_map/kqbfn,kqnrj->krbfj/dot_general | solution.py:63
  417.4 21.4 %fusion.12 = (f32[32,32,128]{2,1,0:T(8,128)S(1)}, f32[32,32,128]{2,1,0:T(8,128)S(1)}) fusion(f32[32,64,128]{2,1,0:T(8,128)S(1)} %slice_bitcast_fusion.10, bf16[32,2,32,64,128]{4,3,2,1,0:T(8,128)(2,1)} %fusion.10), kind=kLoop, calls=%fused_computation.58 | loop fusion | flops 83623936 | bytes 35651584 | tf_op jit(solution)/shard_map/reduce_sum | solution.py:86
  440.5 61.3 %all-reduce.10.cloned.1.call-done = f32[32,64,128]{2,1,0:T(8,128)} async-done(((f32[32,64,128]{2,1,0:T(8,128)}), f32[32,64,128]{2,1,0:T(8,128)}) %all-reduce.10.cloned.1.call-update) | async-done | bytes 1048592 | tf_op jit(solution)/shard_map/psum | solution.py:91
  503.0 18.9 %fusion.16 = (f32[32,64,128]{2,1,0:T(8,128)S(1)}, f32[32,64,128]{2,1,0:T(8,128)S(1)}, f32[32,64,128]{2,1,0:T(8,128)S(1)}) fusion(f32[32,32,128]{2,1,0:T(8,128)S(1)} %get-tuple-element.55, f32[32,32,128]{2,1,0:T(8,128)S(1)} %get-tuple-element.54, bf16[32,2,32,64,128]{4,3,2,1,0:T(8,128)(2,1)} %fusion.10), kind=kLoop, calls=%fused_computation.62 | loop fusion | flops 116654080 | bytes 37748736 | tf_op jit(solution)/shard_map/reduce_sum | solution.py:97
  524.3 68.7 %all-reduce.12.cloned.1.call-done = f32[2,32,64,128]{3,2,1,0:T(8,128)} async-done(((f32[2,32,64,128]{3,2,1,0:T(8,128)}), f32[2,32,64,128]{3,2,1,0:T(8,128)}) %all-reduce.12.cloned.1.call-update) | async-done | bytes 2097168 | tf_op jit(solution)/shard_map/psum | solution.py:103
  596.7 21.2 %fusion.22 = (f32[32,32,128]{2,1,0:T(8,128)S(1)}, f32[32,32,128]{2,1,0:T(8,128)S(1)}) fusion(f32[32,64,128]{2,1,0:T(8,128)S(1)} %get-tuple-element.43, f32[32,64,128]{2,1,0:T(8,128)S(1)} %get-tuple-element.42, bf16[32,2,32,64,128]{4,3,2,1,0:T(8,128)(2,1)} %fusion.10), kind=kLoop, calls=%fused_computation.68 | loop fusion | flops 83623936 | bytes 36700160 | tf_op jit(solution)/shard_map/reduce_sum | solution.py:86
  619.2 60.0 %all-reduce.14.cloned.1.call-done = f32[32,65,128]{2,1,0:T(8,128)} async-done(((f32[32,65,128]{2,1,0:T(8,128)}), f32[32,65,128]{2,1,0:T(8,128)}) %all-reduce.14.cloned.1.call-update) | async-done | bytes 1064976 | tf_op jit(solution)/shard_map/psum | solution.py:91
  681.7 16.5 %fusion.26 = (f32[32,64,128]{2,1,0:T(8,128)S(1)}, f32[32,64,128]{2,1,0:T(8,128)S(1)}) fusion(f32[32,32,128]{2,1,0:T(8,128)S(1)} %get-tuple-element.53, f32[32,32,128]{2,1,0:T(8,128)S(1)} %get-tuple-element.52, bf16[32,2,32,64,128]{4,3,2,1,0:T(8,128)(2,1)} %fusion.10), kind=kLoop, calls=%fused_computation.72 | loop fusion | flops 83361792 | bytes 36700160 | tf_op jit(solution)/shard_map/reduce_sum | solution.py:97
  700.7 68.4 %all-reduce.16.cloned.1.call-done = f32[2,32,64,128]{3,2,1,0:T(8,128)} async-done(((f32[2,32,64,128]{3,2,1,0:T(8,128)}), f32[2,32,64,128]{3,2,1,0:T(8,128)}) %all-reduce.16.cloned.1.call-update) | async-done | bytes 2097168 | tf_op jit(solution)/shard_map/psum | solution.py:103
  772.9 21.2 %fusion.30 = (f32[32,32,128]{2,1,0:T(8,128)S(1)}, f32[32,32,128]{2,1,0:T(8,128)S(1)}) fusion(f32[32,64,128]{2,1,0:T(8,128)S(1)} %get-tuple-element.41, f32[32,64,128]{2,1,0:T(8,128)S(1)} %get-tuple-element.40, bf16[32,2,32,64,128]{4,3,2,1,0:T(8,128)(2,1)} %fusion.10), kind=kLoop, calls=%fused_computation.76 | loop fusion | flops 83623936 | bytes 36700160 | tf_op jit(solution)/shard_map/reduce_sum | solution.py:86
  795.3 60.0 %all-reduce.18.cloned.1.call-done = f32[32,65,128]{2,1,0:T(8,128)} async-done(((f32[32,65,128]{2,1,0:T(8,128)}), f32[32,65,128]{2,1,0:T(8,128)}) %all-reduce.18.cloned.1.call-update) | async-done | bytes 1064976 | tf_op jit(solution)/shard_map/psum | solution.py:91
  857.8 16.5 %fusion.34 = (f32[32,64,128]{2,1,0:T(8,128)S(1)}, f32[32,64,128]{2,1,0:T(8,128)S(1)}) fusion(f32[32,32,128]{2,1,0:T(8,128)S(1)} %get-tuple-element.51, f32[32,32,128]{2,1,0:T(8,128)S(1)} %get-tuple-element.50, bf16[32,2,32,64,128]{4,3,2,1,0:T(8,128)(2,1)} %fusion.10), kind=kLoop, calls=%fused_computation.80 | loop fusion | flops 83361792 | bytes 36700160 | tf_op jit(solution)/shard_map/reduce_sum | solution.py:97
  876.7 68.6 %all-reduce.20.cloned.1.call-done = f32[2,32,64,128]{3,2,1,0:T(8,128)} async-done(((f32[2,32,64,128]{3,2,1,0:T(8,128)}), f32[2,32,64,128]{3,2,1,0:T(8,128)}) %all-reduce.20.cloned.1.call-update) | async-done | bytes 2097168 | tf_op jit(solution)/shard_map/psum | solution.py:103
  949.0 21.2 %fusion.38 = (f32[32,32,128]{2,1,0:T(8,128)S(1)}, f32[32,32,128]{2,1,0:T(8,128)S(1)}) fusion(f32[32,64,128]{2,1,0:T(8,128)S(1)} %get-tuple-element.39, f32[32,64,128]{2,1,0:T(8,128)S(1)} %get-tuple-element.38, bf16[32,2,32,64,128]{4,3,2,1,0:T(8,128)(2,1)} %fusion.10), kind=kLoop, calls=%fused_computation.84 | loop fusion | flops 83623936 | bytes 36700160 | tf_op jit(solution)/shard_map/reduce_sum | solution.py:86
  971.5 60.0 %all-reduce.22.cloned.1.call-done = f32[32,65,128]{2,1,0:T(8,128)} async-done(((f32[32,65,128]{2,1,0:T(8,128)}), f32[32,65,128]{2,1,0:T(8,128)}) %all-reduce.22.cloned.1.call-update) | async-done | bytes 1064976 | tf_op jit(solution)/shard_map/psum | solution.py:91
  1034.0 16.5 %fusion.42 = (f32[32,64,128]{2,1,0:T(8,128)S(1)}, f32[32,64,128]{2,1,0:T(8,128)S(1)}) fusion(f32[32,32,128]{2,1,0:T(8,128)S(1)} %get-tuple-element.49, f32[32,32,128]{2,1,0:T(8,128)S(1)} %get-tuple-element.48, bf16[32,2,32,64,128]{4,3,2,1,0:T(8,128)(2,1)} %fusion.10), kind=kLoop, calls=%fused_computation.88 | loop fusion | flops 83361792 | bytes 36700160 | tf_op jit(solution)/shard_map/reduce_sum | solution.py:97
  1053.0 68.4 %all-reduce.24.cloned.1.call-done = f32[2,32,64,128]{3,2,1,0:T(8,128)} async-done(((f32[2,32,64,128]{3,2,1,0:T(8,128)}), f32[2,32,64,128]{3,2,1,0:T(8,128)}) %all-reduce.24.cloned.1.call-update) | async-done | bytes 2097168 | tf_op jit(solution)/shard_map/psum | solution.py:103
  1125.2 21.2 %fusion.46 = (f32[32,32,128]{2,1,0:T(8,128)S(1)}, f32[32,32,128]{2,1,0:T(8,128)S(1)}) fusion(f32[32,64,128]{2,1,0:T(8,128)S(1)} %get-tuple-element.37, f32[32,64,128]{2,1,0:T(8,128)S(1)} %get-tuple-element.36, bf16[32,2,32,64,128]{4,3,2,1,0:T(8,128)(2,1)} %fusion.10), kind=kLoop, calls=%fused_computation.92 | loop fusion | flops 83623936 | bytes 36700160 | tf_op jit(solution)/shard_map/reduce_sum | solution.py:86
  1147.6 60.0 %all-reduce.26.cloned.1.call-done = f32[32,65,128]{2,1,0:T(8,128)} async-done(((f32[32,65,128]{2,1,0:T(8,128)}), f32[32,65,128]{2,1,0:T(8,128)}) %all-reduce.26.cloned.1.call-update) | async-done | bytes 1064976 | tf_op jit(solution)/shard_map/psum | solution.py:91
  1210.2 16.5 %fusion.50 = (f32[32,64,128]{2,1,0:T(8,128)S(1)}, f32[32,64,128]{2,1,0:T(8,128)S(1)}) fusion(f32[32,32,128]{2,1,0:T(8,128)S(1)} %get-tuple-element.47, f32[32,32,128]{2,1,0:T(8,128)S(1)} %get-tuple-element.46, bf16[32,2,32,64,128]{4,3,2,1,0:T(8,128)(2,1)} %fusion.10), kind=kLoop, calls=%fused_computation.96 | loop fusion | flops 83361792 | bytes 36700160 | tf_op jit(solution)/shard_map/reduce_sum | solution.py:97
  1227.5 4.4 copy.47
  1232.0 51.8 %reduce-scatter.2.cloned.1.call-done = f32[2,1024,64]{2,1,0:T(8,128)} async-done(((f32[2,4096,64]{2,1,0:T(8,128)}), f32[2,1024,64]{2,1,0:T(8,128)}) %reduce-scatter.2.cloned.1.call-update) | async-done | bytes 524304 | tf_op jit(solution)/shard_map/reduce_scatter | solution.py:105
  1286.9 20.0 %all_to_all.36 = f32[8,1,16384]{2,1,0:T(1,128)S(1)} all-to-all(f32[8,1,16384]{2,1,0:T(1,128)S(1)} %reshape.301), channel_id=1, replica_groups=mesh['section'=4,'chan'=8] {'chan'}, dimensions={0} | all-to-all | bytes 1048576 | tf_op jit(solution)/shard_map/all_to_all | solution.py:106
  (105 shorter events, 70.3 us)
Async XLA Ops:
  10.3 89.4 %collective-permute-start = (bf16[2,64,12288]{2,1,0:T(8,128)(2,1)}, bf16[2,64,12288]{2,1,0:T(8,128)(2,1)}, u32[]{:S(2)}, u32[]{:S(2)}) collective-permute-start(bf16[2,64,12288]{2,1,0:T(8,128)(2,1)} %slice.103), channel_id=1, source_target_pairs={{0,8},{8,16},{16,24},{1,9},{9,17},{17,25},{2,10},{10,18},{18,26},{... | collective-permute-start | bytes 9437192 | tf_op jit(solution)/shard_map/ppermute | solution.py:17
  20.4 20.2 %all-to-all-start = ((f32[2,128,512]{1,0,2:T(2,128)}), f32[2,128,512]{1,0,2:T(2,128)S(1)}, u32[]{:S(2)}, u32[]{:S(2)}) async-start(f32[2,128,512]{1,0,2:T(2,128)} %pad_maximum_fusion.9), calls=%async_computation | async-start | bytes 1048576 | tf_op jit(solution)/shard_map/all_to_all | solution.py:73
  25.2 384.4 %all-gather.2.cloned.1.call-start = ((), (), s32[]{:S(2)}) async-start(), calls=%async_computation.3 | async-start | bytes 2621440 | tf_op jit(solution)/shard_map/all_gather | solution.py:74
  41.5 460.2 %all-reduce.10.cloned.1.call-start = ((), (), s32[]{:S(2)}) async-start(), calls=%async_computation.4 | async-start | bytes 2097152 | tf_op jit(solution)/shard_map/psum | solution.py:91
  440.0 153.0 %all-reduce.12.cloned.1.call-start = ((), (), s32[]{:S(2)}) async-start(), calls=%async_computation.5 | async-start | bytes 4194304 | tf_op jit(solution)/shard_map/psum | solution.py:103
  524.3 154.9 %all-reduce.14.cloned.1.call-start = ((), (), s32[]{:S(2)}) async-start(), calls=%async_computation.6 | async-start | bytes 2359296 | tf_op jit(solution)/shard_map/psum | solution.py:91
  619.1 150.0 %all-reduce.16.cloned.1.call-start = ((), (), s32[]{:S(2)}) async-start(), calls=%async_computation.7 | async-start | bytes 4194304 | tf_op jit(solution)/shard_map/psum | solution.py:103
  679.1 19.0 %copy-start.1 = (f32[2,32,64,128]{3,2,1,0:T(8,128)S(1)}, f32[2,32,64,128]{3,2,1,0:T(8,128)}, u32[]{:S(2)}) copy-start(f32[2,32,64,128]{3,2,1,0:T(8,128)} %all-reduce.12.cloned.1.call-done) | copy-start | bytes 6291460
  700.5 154.8 %all-reduce.18.cloned.1.call-start = ((), (), s32[]{:S(2)}) async-start(), calls=%async_computation.8 | async-start | bytes 2359296 | tf_op jit(solution)/shard_map/psum | solution.py:91
  795.3 150.0 %all-reduce.20.cloned.1.call-start = ((), (), s32[]{:S(2)}) async-start(), calls=%async_computation.9 | async-start | bytes 4194304 | tf_op jit(solution)/shard_map/psum | solution.py:103
  855.3 19.0 %copy-start.2 = (f32[2,32,64,128]{3,2,1,0:T(8,128)S(1)}, f32[2,32,64,128]{3,2,1,0:T(8,128)}, u32[]{:S(2)}) copy-start(f32[2,32,64,128]{3,2,1,0:T(8,128)} %all-reduce.16.cloned.1.call-done) | copy-start | bytes 6291460
  876.6 154.8 %all-reduce.22.cloned.1.call-start = ((), (), s32[]{:S(2)}) async-start(), calls=%async_computation.10 | async-start | bytes 2359296 | tf_op jit(solution)/shard_map/psum | solution.py:91
  971.4 150.0 %all-reduce.24.cloned.1.call-start = ((), (), s32[]{:S(2)}) async-start(), calls=%async_computation.11 | async-start | bytes 4194304 | tf_op jit(solution)/shard_map/psum | solution.py:103
  1031.4 19.0 %copy-start.3 = (f32[2,32,64,128]{3,2,1,0:T(8,128)S(1)}, f32[2,32,64,128]{3,2,1,0:T(8,128)}, u32[]{:S(2)}) copy-start(f32[2,32,64,128]{3,2,1,0:T(8,128)} %all-reduce.20.cloned.1.call-done) | copy-start | bytes 6291460
  1052.8 154.8 %all-reduce.26.cloned.1.call-start = ((), (), s32[]{:S(2)}) async-start(), calls=%async_computation.12 | async-start | bytes 2359296 | tf_op jit(solution)/shard_map/psum | solution.py:91
  1147.6 136.2 %reduce-scatter.2.cloned.1.call-start = ((), (), s32[]{:S(2)}) async-start(), calls=%async_computation.13 | async-start | bytes 5242880 | tf_op jit(solution)/shard_map/reduce_scatter | solution.py:105
  1207.6 19.0 %copy-start = (f32[2,32,64,128]{3,2,1,0:T(8,128)S(1)}, f32[2,32,64,128]{3,2,1,0:T(8,128)}, u32[]{:S(2)}) copy-start(f32[2,32,64,128]{3,2,1,0:T(8,128)} %all-reduce.24.cloned.1.call-done) | copy-start | bytes 6291460
Sparse Core Ops, SparseCore 0:
  41.6 49.6 all-gather.1
  440.1 61.5 all-reduce.9
  524.4 68.5 all-reduce.11
  619.3 59.8 all-reduce.13
  700.6 68.5 all-reduce.15
  795.4 59.8 all-reduce.17
  876.7 68.5 all-reduce.19
  971.6 59.8 all-reduce.21
  1052.9 68.5 all-reduce.23
  1147.7 59.8 all-reduce.25
  1232.1 51.6 reduce-scatter.1
where the time goes:
time: 1330 us; the launch traced here: 1320 us
  waiting for transfers between devices  687 us (52%)
  other arithmetic  276 us (21%)
  matrix products  178 us (13%)
  local copies, waits for them, and re-layouts  131 us (10%)
  blocking collectives  20 us (2%)
  between operations  14 us (1%)
    psum x5, waiting for transfers between devices, local(): rows = lax.psum(jnp.concatenate(rows, axis=1), 'chan')  301 us
    psum x4, waiting for transfers between devices, local(): now_r, now_i = lax.psum(result, 'section')  274 us
    dot_general x1, matrix products, channelize(): jnp.einsum('pmbfn,pmqk->kqbfn', filtered, first_table(outer), precision=l...  112 us
    reduce_sum x5, other arithmetic, local(): proj_r = jnp.sum(real * ur + imag * ui, axis=2)  106 us
    reduce_sum x5, other arithmetic, local(): back_r = jnp.sum(real * pr - imag * pi, axis=1)  84.8 us
    dot_general x1, matrix products, channelize(): jnp.einsum('kqbfn,kqnrj->krbfj', halfway, table, precision=lax.Precision....  65.4 us
    ppermute x1, waiting for transfers between devices, shifted_2(): return lax.ppermute(block, axis, route)  58 us
    unnamed x17, local copies, waits for them, and re-layouts  53 us
  transfers between devices with their start and end apart: 13, of which 12 were waited for; matrix products, arithmetic and copies ran while one was open for 25% of the time, Pallas kernels for 0%

commit v1 on v0

--- a/solution.py
+++ b/solution.py
@@ -88,7 +88,7 @@
         rows = [proj_r, proj_i]
         if iteration > 0:
             rows.append(jnp.sum(now_r * now_r + now_i * now_i, axis=1)[:, None])
-        rows = lax.psum(jnp.concatenate(rows, axis=1), "chan")
+        rows = jnp.sum(lax.all_gather(jnp.concatenate(rows, axis=1), "chan"), axis=0)
         if iteration > 0:
             inverse = 1.0 / jnp.sqrt(rows[:, 2 * blocks :] + epsilon)
             rows = rows[:, : 2 * blocks] * inverse

time: 1330 us -> 1460 us (1.098)
  waiting for transfers between devices: 687 us -> 797 us
  other arithmetic: 276 us -> 295 us
    all_gather x0 -> x5, waiting for transfers between devices: none -> 416 us  [local(): lax.all_gather(jnp.concatenate(rows, axis=1), 'chan')]
    psum x5 -> x0, waiting for transfers between devices: 301 us -> none  [local(): rows = lax.psum(jnp.concatenate(rows, axis=1), 'chan')]
    reduce_sum x0 -> x5, other arithmetic: none -> 26.9 us  [local(): jnp.sum(lax.all_gather(jnp.concatenate(rows, axis=1), 'chan'), axis=0)]
    unnamed x17 -> x21, local copies, waits for them, and re-layouts: 53 us -> 52.7 us
  transfers between devices with their start and end apart: 13 -> 13, of which waited for: 12 -> 12; matrix products, arithmetic and copies ran while one was open for 25% -> 23% of each run, Pallas kernels for 0% -> 0%
where the time goes in v1:
time: 1460 us; the launch traced here: 1450 us
  waiting for transfers between devices  797 us (55%)
  other arithmetic  295 us (20%)
  matrix products  178 us (12%)
  local copies, waits for them, and re-layouts  136 us (9%)
  blocking collectives  19.7 us (1%)
    all_gather x5, waiting for transfers between devices, local(): lax.all_gather(jnp.concatenate(rows, axis=1), 'chan')  416 us
    psum x4, waiting for transfers between devices, local(): now_r, now_i = lax.psum(result, 'section')  272 us
    dot_general x1, matrix products, channelize(): jnp.einsum('pmbfn,pmqk->kqbfn', filtered, first_table(outer), precision=l...  112 us
    reduce_sum x5, other arithmetic, local(): proj_r = jnp.sum(real * ur + imag * ui, axis=2)  107 us
    reduce_sum x5, other arithmetic, local(): back_r = jnp.sum(real * pr - imag * pi, axis=1)  85.3 us
    dot_general x1, matrix products, channelize(): jnp.einsum('kqbfn,kqnrj->krbfj', halfway, table, precision=lax.Precision....  65.5 us
    ppermute x1, waiting for transfers between devices, shifted_2(): return lax.ppermute(block, axis, route)  54.9 us
    unnamed x21, local copies, waits for them, and re-layouts  52.7 us
  transfers between devices with their start and end apart: 13, of which 12 were waited for; matrix products, arithmetic and copies ran while one was open for 23% of the time, Pallas kernels for 0%

profile of v1, /device:TPU:0, one launch (start us, length us, event | category | flops | bytes accessed | tf_op | source)
XLA Modules:
  0.0 1452.2 jit_solution(7291310825981093472)
XLA Ops:
  8.6 6.6 collective-permute-start
  25.9 8.4 fusion.81
  42.8 54.9 %collective-permute-done = bf16[2,64,12288]{2,1,0:T(8,128)(2,1)} collective-permute-done((bf16[2,64,12288]{2,1,0:T(8,128)(2,1)S(1)}, bf16[2,64,12288]{2,1,0:T(8,128)(2,1)}, u32[]{:S(2)}, u32[]{:S(2)}) %collective-permute-start) | collective-permute-done | bytes 3145760 | tf_op jit(solution)/shard_map/ppermute | solution.py:17
  97.7 35.9 %maximum_convert_fusion = f32[2,64,143360]{2,1,0:T(8,128)} fusion(bf16[2,64,131072]{2,1,0:T(8,128)(2,1)} %param.3, bf16[2,64,12288]{2,1,0:T(8,128)(2,1)} %collective-permute-done), kind=kLoop, calls=%fused_computation.55 | loop fusion | flops 73400320 | bytes 110100480 | tf_op jit(solution)/shard_map/convert_element_type | solution.py:54
  133.6 48.6 %copy.103 = f32[16,8,1120,128]{3,2,1,0:T(8,128)} copy(f32[16,8,1120,128]{3,1,2,0:T(8,128)} %bitcast.85) | data formatting | bytes 146800640
  182.3 47.7 %copy.112 = f32[2,64,35,32,128]{4,3,0,1,2:T(8,128)} copy(f32[2,64,35,32,128]{4,3,2,1,0:T(8,128)} %bitcast.87) | data formatting | bytes 146800640 | tf_op jit(solution)/shard_map/convert_element_type | solution.py:54
  230.0 112.3 %fusion.57 = f32[32,2,32,64,128,1]{4,0,3,2,1,5:T(8,128)} fusion(f32[2,32,35,64,128]{4,1,0,3,2:T(8,128)} %bitcast.278, f32[32,128]{1,0:T(8,128)S(1)} %get-tuple-element.57, f32[32,128]{1,0:T(8,128)S(1)} %get-tuple-element.58, f32[32,128]{1,0:T(8,128)S(1)} %get-tuple-element.59, f32[32,128]{1,0:T(8,128)S(1)} %get-tuple-element.56, ...), kind=kOutput, calls=%fused_computation.103 | convolution fusion | flops 6559895552 | bytes 335626240 | tf_op jit(solution)/shard_map/pmbfn,pmqk->kqbfn/dot_general | solution.py:59
  342.3 65.5 %fusion.10 = bf16[32,2,32,64,128]{4,3,2,1,0:T(8,128)(2,1)} fusion(f32[32,2,32,64,128,1]{4,0,3,2,1,5:T(8,128)} %fusion.57, f32[32,1,128,2,128]{4,2,1,3,0:T(8,128)} %get-tuple-element.45, f32[32,1,128,2,128]{4,2,1,3,0:T(8,128)} %get-tuple-element.44), kind=kOutput, calls=%fused_computation.56 | convolution fusion | flops 25788678144 | bytes 109051904 | tf_op jit(solution)/shard_map/kqbfn,kqnrj->krbfj/dot_general | solution.py:63
  415.5 21.5 %fusion.12 = (f32[32,32,128]{2,1,0:T(8,128)S(1)}, f32[32,32,128]{2,1,0:T(8,128)S(1)}) fusion(f32[32,64,128]{2,1,0:T(8,128)S(1)} %slice_bitcast_fusion.10, bf16[32,2,32,64,128]{4,3,2,1,0:T(8,128)(2,1)} %fusion.10), kind=kLoop, calls=%fused_computation.58 | loop fusion | flops 83623936 | bytes 35651584 | tf_op jit(solution)/shard_map/reduce_sum | solution.py:86
  438.6 84.0 %all-gather.14.cloned.1.call-done = f32[256,64,128]{2,1,0:T(8,128)} async-done(((f32[32,64,128]{2,1,0:T(8,128)}), f32[256,64,128]{2,1,0:T(8,128)}) %all-gather.14.cloned.1.call-update) | async-done | bytes 8388624 | tf_op jit(solution)/shard_map/all_gather | solution.py:91
  527.1 18.9 %fusion.16 = (f32[32,64,128]{2,1,0:T(8,128)S(1)}, f32[32,64,128]{2,1,0:T(8,128)S(1)}, f32[32,64,128]{2,1,0:T(8,128)S(1)}) fusion(f32[32,32,128]{2,1,0:T(8,128)S(1)} %get-tuple-element.55, f32[32,32,128]{2,1,0:T(8,128)S(1)} %get-tuple-element.54, bf16[32,2,32,64,128]{4,3,2,1,0:T(8,128)(2,1)} %fusion.10), kind=kLoop, calls=%fused_computation.62 | loop fusion | flops 116654080 | bytes 37748736 | tf_op jit(solution)/shard_map/reduce_sum | solution.py:97
  548.5 68.1 %all-reduce.5.cloned.1.call-done = f32[2,32,64,128]{3,2,1,0:T(8,128)} async-done(((f32[2,32,64,128]{3,2,1,0:T(8,128)}), f32[2,32,64,128]{3,2,1,0:T(8,128)}) %all-reduce.5.cloned.1.call-update) | async-done | bytes 2097168 | tf_op jit(solution)/shard_map/psum | solution.py:103
  618.3 21.4 %fusion.22 = (f32[32,32,128]{2,1,0:T(8,128)S(1)}, f32[32,32,128]{2,1,0:T(8,128)S(1)}) fusion(f32[32,64,128]{2,1,0:T(8,128)S(1)} %get-tuple-element.43, f32[32,64,128]{2,1,0:T(8,128)S(1)} %get-tuple-element.42, bf16[32,2,32,64,128]{4,3,2,1,0:T(8,128)(2,1)} %fusion.10), kind=kLoop, calls=%fused_computation.68 | loop fusion | flops 83623936 | bytes 36700160 | tf_op jit(solution)/shard_map/reduce_sum | solution.py:86
  641.5 83.0 %all-gather.16.cloned.1.call-done = f32[256,65,128]{2,0,1:T(8,128)} async-done(((f32[32,65,128]{2,0,1:T(8,128)}), f32[256,65,128]{2,0,1:T(8,128)}) %all-gather.16.cloned.1.call-update) | async-done | bytes 8519696 | tf_op jit(solution)/shard_map/all_gather | solution.py:91
  724.5 5.6 reduce_sum.313
  732.9 16.6 %fusion.26 = (f32[32,64,128]{2,1,0:T(8,128)S(1)}, f32[32,64,128]{2,1,0:T(8,128)S(1)}) fusion(f32[32,32,128]{2,1,0:T(8,128)S(1)} %copy.67, f32[32,32,128]{2,1,0:T(8,128)S(1)} %copy.66, bf16[32,2,32,64,128]{4,3,2,1,0:T(8,128)(2,1)} %fusion.10), kind=kLoop, calls=%fused_computation.72 | loop fusion | flops 83361792 | bytes 36700160 | tf_op jit(solution)/shard_map/reduce_sum | solution.py:97
  752.0 68.1 %all-reduce.7.cloned.1.call-done = f32[2,32,64,128]{3,2,1,0:T(8,128)} async-done(((f32[2,32,64,128]{3,2,1,0:T(8,128)}), f32[2,32,64,128]{3,2,1,0:T(8,128)}) %all-reduce.7.cloned.1.call-update) | async-done | bytes 2097168 | tf_op jit(solution)/shard_map/psum | solution.py:103
  821.9 21.4 %fusion.30 = (f32[32,32,128]{2,1,0:T(8,128)S(1)}, f32[32,32,128]{2,1,0:T(8,128)S(1)}) fusion(f32[32,64,128]{2,1,0:T(8,128)S(1)} %get-tuple-element.41, f32[32,64,128]{2,1,0:T(8,128)S(1)} %get-tuple-element.40, bf16[32,2,32,64,128]{4,3,2,1,0:T(8,128)(2,1)} %fusion.10), kind=kLoop, calls=%fused_computation.76 | loop fusion | flops 83623936 | bytes 36700160 | tf_op jit(solution)/shard_map/reduce_sum | solution.py:86
  845.0 83.0 %all-gather.18.cloned.1.call-done = f32[256,65,128]{2,0,1:T(8,128)} async-done(((f32[32,65,128]{2,0,1:T(8,128)}), f32[256,65,128]{2,0,1:T(8,128)}) %all-gather.18.cloned.1.call-update) | async-done | bytes 8519696 | tf_op jit(solution)/shard_map/all_gather | solution.py:91
  928.0 5.6 reduce_sum.321
  936.4 16.6 %fusion.34 = (f32[32,64,128]{2,1,0:T(8,128)S(1)}, f32[32,64,128]{2,1,0:T(8,128)S(1)}) fusion(f32[32,32,128]{2,1,0:T(8,128)S(1)} %copy.72, f32[32,32,128]{2,1,0:T(8,128)S(1)} %copy.71, bf16[32,2,32,64,128]{4,3,2,1,0:T(8,128)(2,1)} %fusion.10), kind=kLoop, calls=%fused_computation.80 | loop fusion | flops 83361792 | bytes 36700160 | tf_op jit(solution)/shard_map/reduce_sum | solution.py:97
  955.5 68.1 %all-reduce.9.cloned.1.call-done = f32[2,32,64,128]{3,2,1,0:T(8,128)} async-done(((f32[2,32,64,128]{3,2,1,0:T(8,128)}), f32[2,32,64,128]{3,2,1,0:T(8,128)}) %all-reduce.9.cloned.1.call-update) | async-done | bytes 2097168 | tf_op jit(solution)/shard_map/psum | solution.py:103
  1025.4 21.4 %fusion.38 = (f32[32,32,128]{2,1,0:T(8,128)S(1)}, f32[32,32,128]{2,1,0:T(8,128)S(1)}) fusion(f32[32,64,128]{2,1,0:T(8,128)S(1)} %get-tuple-element.39, f32[32,64,128]{2,1,0:T(8,128)S(1)} %get-tuple-element.38, bf16[32,2,32,64,128]{4,3,2,1,0:T(8,128)(2,1)} %fusion.10), kind=kLoop, calls=%fused_computation.84 | loop fusion | flops 83623936 | bytes 36700160 | tf_op jit(solution)/shard_map/reduce_sum | solution.py:86
  1048.6 83.0 %all-gather.20.cloned.1.call-done = f32[256,65,128]{2,0,1:T(8,128)} async-done(((f32[32,65,128]{2,0,1:T(8,128)}), f32[256,65,128]{2,0,1:T(8,128)}) %all-gather.20.cloned.1.call-update) | async-done | bytes 8519696 | tf_op jit(solution)/shard_map/all_gather | solution.py:91
  1131.6 5.6 reduce_sum.329
  1140.0 16.6 %fusion.42 = (f32[32,64,128]{2,1,0:T(8,128)S(1)}, f32[32,64,128]{2,1,0:T(8,128)S(1)}) fusion(f32[32,32,128]{2,1,0:T(8,128)S(1)} %copy.77, f32[32,32,128]{2,1,0:T(8,128)S(1)} %copy.76, bf16[32,2,32,64,128]{4,3,2,1,0:T(8,128)(2,1)} %fusion.10), kind=kLoop, calls=%fused_computation.88 | loop fusion | flops 83361792 | bytes 36700160 | tf_op jit(solution)/shard_map/reduce_sum | solution.py:97
  1159.1 68.1 %all-reduce.11.cloned.1.call-done = f32[2,32,64,128]{3,2,1,0:T(8,128)} async-done(((f32[2,32,64,128]{3,2,1,0:T(8,128)}), f32[2,32,64,128]{3,2,1,0:T(8,128)}) %all-reduce.11.cloned.1.call-update) | async-done | bytes 2097168 | tf_op jit(solution)/shard_map/psum | solution.py:103
  1228.9 21.4 %fusion.46 = (f32[32,32,128]{2,1,0:T(8,128)S(1)}, f32[32,32,128]{2,1,0:T(8,128)S(1)}) fusion(f32[32,64,128]{2,1,0:T(8,128)S(1)} %get-tuple-element.37, f32[32,64,128]{2,1,0:T(8,128)S(1)} %get-tuple-element.36, bf16[32,2,32,64,128]{4,3,2,1,0:T(8,128)(2,1)} %fusion.10), kind=kLoop, calls=%fused_computation.92 | loop fusion | flops 83623936 | bytes 36700160 | tf_op jit(solution)/shard_map/reduce_sum | solution.py:86
  1252.2 82.9 %all-gather.22.cloned.1.call-done = f32[256,65,128]{2,0,1:T(8,128)} async-done(((f32[32,65,128]{2,0,1:T(8,128)}), f32[256,65,128]{2,0,1:T(8,128)}) %all-gather.22.cloned.1.call-update) | async-done | bytes 8519696 | tf_op jit(solution)/shard_map/all_gather | solution.py:91
  1343.5 16.6 %fusion.50 = (f32[32,64,128]{2,1,0:T(8,128)S(1)}, f32[32,64,128]{2,1,0:T(8,128)S(1)}) fusion(f32[32,32,128]{2,1,0:T(8,128)S(1)} %copy.82, f32[32,32,128]{2,1,0:T(8,128)S(1)} %copy.81, bf16[32,2,32,64,128]{4,3,2,1,0:T(8,128)(2,1)} %fusion.10), kind=kLoop, calls=%fused_computation.96 | loop fusion | flops 83361792 | bytes 36700160 | tf_op jit(solution)/shard_map/reduce_sum | solution.py:97
  1365.8 51.2 %reduce-scatter.2.cloned.1.call-done = f32[2,1024,64]{2,1,0:T(8,128)} async-done(((f32[2,4096,64]{2,1,0:T(8,128)}), f32[2,1024,64]{2,1,0:T(8,128)}) %reduce-scatter.2.cloned.1.call-update) | async-done | bytes 524304 | tf_op jit(solution)/shard_map/reduce_scatter | solution.py:105
  1420.2 19.7 %all_to_all.36 = f32[8,1,16384]{2,1,0:T(1,128)S(1)} all-to-all(f32[8,1,16384]{2,1,0:T(1,128)S(1)} %reshape.306), channel_id=1, replica_groups=mesh['section'=4,'chan'=8] {'chan'}, dimensions={0} | all-to-all | bytes 1048576 | tf_op jit(solution)/shard_map/all_to_all | solution.py:106
  (122 shorter events, 89.7 us)
Async XLA Ops:
  8.6 89.1 %collective-permute-start = (bf16[2,64,12288]{2,1,0:T(8,128)(2,1)S(1)}, bf16[2,64,12288]{2,1,0:T(8,128)(2,1)}, u32[]{:S(2)}, u32[]{:S(2)}) collective-permute-start(bf16[2,64,12288]{2,1,0:T(8,128)(2,1)S(1)} %slice.103), channel_id=1, source_target_pairs={{0,8},{8,16},{16,24},{1,9},{9,17},{17,25},{2,10},{10,18},{18,26},{... | collective-permute-start | bytes 9437192 | tf_op jit(solution)/shard_map/ppermute | solution.py:17
  20.3 20.3 %all-to-all-start = ((f32[2,128,512]{1,0,2:T(2,128)}), f32[2,128,512]{1,0,2:T(2,128)}, u32[]{:S(2)}, u32[]{:S(2)}) async-start(f32[2,128,512]{1,0,2:T(2,128)} %pad_maximum_fusion.9), calls=%async_computation | async-start | bytes 1048576 | tf_op jit(solution)/shard_map/all_to_all | solution.py:73
  25.2 382.6 %all-gather.12.cloned.1.call-start = ((), (), s32[]{:S(2)}) async-start(), calls=%async_computation.3 | async-start | bytes 2621440 | tf_op jit(solution)/shard_map/all_gather | solution.py:74
  42.6 480.1 %all-gather.14.cloned.1.call-start = ((), (), s32[]{:S(2)}) async-start(), calls=%async_computation.9 | async-start | bytes 9437184 | tf_op jit(solution)/shard_map/all_gather | solution.py:91
  438.1 178.4 %all-reduce.5.cloned.1.call-start = ((), (), s32[]{:S(2)}) async-start(), calls=%async_computation.4 | async-start | bytes 4194304 | tf_op jit(solution)/shard_map/psum | solution.py:103
  548.4 176.1 %all-gather.16.cloned.1.call-start = ((), (), s32[]{:S(2)}) async-start(), calls=%async_computation.10 | async-start | bytes 9584640 | tf_op jit(solution)/shard_map/all_gather | solution.py:91
  618.3 21.4 %copy-start.2 = (f32[2,32,64,128]{3,2,1,0:T(8,128)S(1)}, f32[2,32,64,128]{3,2,1,0:T(8,128)}, u32[]{:S(2)}) copy-start(f32[2,32,64,128]{3,2,1,0:T(8,128)} %all-reduce.5.cloned.1.call-done) | copy-start | bytes 6291460
  641.2 178.8 %all-reduce.7.cloned.1.call-start = ((), (), s32[]{:S(2)}) async-start(), calls=%async_computation.5 | async-start | bytes 4194304 | tf_op jit(solution)/shard_map/psum | solution.py:103
  732.9 16.6 %copy-start.3 = (f32[2,32,64,128]{3,2,1,0:T(8,128)S(1)}, f32[2,32,64,128]{3,2,1,0:T(8,128)}, u32[]{:S(2)}) copy-start(f32[2,32,64,128]{3,2,1,0:T(8,128)} %all-reduce.5.cloned.1.call-done) | copy-start | bytes 6291460
  751.9 176.1 %all-gather.18.cloned.1.call-start = ((), (), s32[]{:S(2)}) async-start(), calls=%async_computation.11 | async-start | bytes 9584640 | tf_op jit(solution)/shard_map/all_gather | solution.py:91
  821.9 21.4 %copy-start.4 = (f32[2,32,64,128]{3,2,1,0:T(8,128)S(1)}, f32[2,32,64,128]{3,2,1,0:T(8,128)}, u32[]{:S(2)}) copy-start(f32[2,32,64,128]{3,2,1,0:T(8,128)} %all-reduce.7.cloned.1.call-done) | copy-start | bytes 6291460
  844.8 178.8 %all-reduce.9.cloned.1.call-start = ((), (), s32[]{:S(2)}) async-start(), calls=%async_computation.6 | async-start | bytes 4194304 | tf_op jit(solution)/shard_map/psum | solution.py:103
  936.4 16.6 %copy-start.5 = (f32[2,32,64,128]{3,2,1,0:T(8,128)S(1)}, f32[2,32,64,128]{3,2,1,0:T(8,128)}, u32[]{:S(2)}) copy-start(f32[2,32,64,128]{3,2,1,0:T(8,128)} %all-reduce.7.cloned.1.call-done) | copy-start | bytes 6291460
  955.5 176.1 %all-gather.20.cloned.1.call-start = ((), (), s32[]{:S(2)}) async-start(), calls=%async_computation.12 | async-start | bytes 9584640 | tf_op jit(solution)/shard_map/all_gather | solution.py:91
  1025.4 21.4 %copy-start.6 = (f32[2,32,64,128]{3,2,1,0:T(8,128)S(1)}, f32[2,32,64,128]{3,2,1,0:T(8,128)}, u32[]{:S(2)}) copy-start(f32[2,32,64,128]{3,2,1,0:T(8,128)} %all-reduce.9.cloned.1.call-done) | copy-start | bytes 6291460
  1048.3 178.8 %all-reduce.11.cloned.1.call-start = ((), (), s32[]{:S(2)}) async-start(), calls=%async_computation.7 | async-start | bytes 4194304 | tf_op jit(solution)/shard_map/psum | solution.py:103
  1140.0 16.6 %copy-start.7 = (f32[2,32,64,128]{3,2,1,0:T(8,128)S(1)}, f32[2,32,64,128]{3,2,1,0:T(8,128)}, u32[]{:S(2)}) copy-start(f32[2,32,64,128]{3,2,1,0:T(8,128)} %all-reduce.9.cloned.1.call-done) | copy-start | bytes 6291460
  1159.0 176.1 %all-gather.22.cloned.1.call-start = ((), (), s32[]{:S(2)}) async-start(), calls=%async_computation.13 | async-start | bytes 9584640 | tf_op jit(solution)/shard_map/all_gather | solution.py:91
  1228.9 21.4 %copy-start = (f32[2,32,64,128]{3,2,1,0:T(8,128)S(1)}, f32[2,32,64,128]{3,2,1,0:T(8,128)}, u32[]{:S(2)}) copy-start(f32[2,32,64,128]{3,2,1,0:T(8,128)} %all-reduce.11.cloned.1.call-done) | copy-start | bytes 6291460
  1251.9 165.2 %reduce-scatter.2.cloned.1.call-start = ((), (), s32[]{:S(2)}) async-start(), calls=%async_computation.8 | async-start | bytes 5242880 | tf_op jit(solution)/shard_map/reduce_scatter | solution.py:105
  1343.5 16.6 %copy-start.1 = (f32[2,32,64,128]{3,2,1,0:T(8,128)S(1)}, f32[2,32,64,128]{3,2,1,0:T(8,128)}, u32[]{:S(2)}) copy-start(f32[2,32,64,128]{3,2,1,0:T(8,128)} %all-reduce.11.cloned.1.call-done) | copy-start | bytes 6291460
Sparse Core Ops, SparseCore 0:
  42.7 49.4 all-gather.11
  438.2 84.3 all-gather.13
  548.5 67.9 all-reduce.4
  641.4 83.0 all-gather.15
  752.1 67.9 all-reduce.6
  844.9 83.0 all-gather.17
  955.6 67.9 all-reduce.8
  1048.4 83.0 all-gather.19
  1159.2 67.9 all-reduce.10
  1252.0 83.0 all-gather.21
  1365.9 51.0 reduce-scatter.1
